TPU v7x, 32 devices: a whole 2x2x4 slice. The times are simulated.
32 devices in a mesh: wide: 4 (over x, core), narrow: 8 (over z, y).
Axes of the slice: x: 2, y: 2, z: 4, core: 2. Of those that a mesh axis runs over, the one named last changes fastest.
Arguments:
- single: bfloat16 [48, 128, 768], P('narrow', 'wide'), may hold values from -6 to 6
- pair: bfloat16 [128, 128, 128], P('wide', 'narrow'), may hold values from -6 to 6
- restype: int32 [128], P('wide'), may hold values from 0 to 31
- chain: int32 [128], replicated, may hold values from 0 to 7, never falling along the last dimension, each value on 1 to 32 neighbouring positions
- residue_type_embedding: float32 [32, 768], replicated, may hold values from -6 to 6
- pair_bias_weight: bfloat16 [2, 16, 128], replicated, may hold values from -41 to 41, as said below
- shared_chain_score: float32 [2, 16], replicated, may hold values from -8 to 8
- query_weight: bfloat16 [2, 768, 768], replicated, may hold values from -0.21875 to 0.21875
- key_weight: bfloat16 [2, 768, 768], replicated, may hold values from -0.21875 to 0.21875
- value_weight: bfloat16 [2, 768, 768], replicated, may hold values from -0.21875 to 0.21875
- output_weight: bfloat16 [2, 768, 768], replicated, may hold values from -0.21875 to 0.21875
Outputs:
- updated: bfloat16 [48, 128, 768], P('narrow', 'wide')
Inputs may be any that keep to these rules, and one draw needn't show every extreme that they name: `pair_bias_weight`: each entry is a real number.
All inputs are finite; a program needn't handle non-finite values.
Results may differ from a plain program's by a relative error of at most 0.0084.
Values may be sent and summed in bfloat16 or wider, within the bound.
No kernel may reach another device: no remote copies, remote signals or barrier semaphores. Data moves between devices by JAX's collectives and lax.ppermute only.
A program may use at most 128 MiB of HBM per device.

v0:
```python
import math
import jax
import jax.numpy as jnp
from jax import lax
from jax.sharding import PartitionSpec as P

epsilon_norm = 1e-05


def normalize(inputs):
    average = jnp.mean(inputs, axis=-1, keepdims=True)
    centered = inputs - average
    spread_squared = jnp.mean(centered * centered, axis=-1, keepdims=True)
    return centered * lax.rsqrt(spread_squared + epsilon_norm)


def attend(stacked, layer_head_bias, score_scale):
    head_dim = stacked.shape[-1] // 3
    queries = stacked[..., :head_dim]
    key_rows = stacked[..., head_dim : 2 * head_dim]
    value_rows = stacked[..., 2 * head_dim :]
    batch_count, row_count, head_count, _ = queries.shape
    running_max = jnp.full((batch_count, head_count, row_count), -jnp.inf, jnp.float32)
    running_sum = jnp.zeros((batch_count, head_count, row_count), jnp.float32)
    running_out = jnp.zeros((batch_count, row_count, head_count, head_dim), jnp.float32)
    key_piece = lax.all_gather(key_rows, "wide", axis=1, tiled=True)
    value_piece = lax.all_gather(value_rows, "wide", axis=1, tiled=True)
    scores = (
        jnp.einsum("aqhd,akhd->ahqk", queries, key_piece, preferred_element_type=jnp.float32)
        * score_scale
        + layer_head_bias[None]
    )
    refreshed_peak = jnp.max(scores, axis=-1)
    rescale = jnp.exp(running_max - refreshed_peak)
    weights_exp = jnp.exp(scores - refreshed_peak[..., None])
    running_sum = running_sum * rescale + jnp.sum(weights_exp, axis=-1)
    contrib = jnp.einsum(
        "ahqk,akhd->aqhd",
        weights_exp.astype(jnp.bfloat16),
        value_piece,
        preferred_element_type=jnp.float32,
    )
    running_out = running_out * jnp.swapaxes(rescale, 1, 2)[..., None] + contrib
    return (running_out / jnp.swapaxes(running_sum, 1, 2)[..., None]).astype(jnp.bfloat16)


def shards(
    single,
    pair,
    restype,
    chain,
    residue_type_embedding,
    pair_bias_weight,
    shared_chain_score,
    query_weight,
    key_weight,
    value_weight,
    output_weight,
):
    sample_count, row_count, model_width = single.shape
    head_count = pair_bias_weight.shape[1]
    head_dim = model_width // head_count
    block_count = query_weight.shape[0]
    row_begin = lax.axis_index("wide") * row_count
    onehot = (
        restype[:, None] == jnp.arange(residue_type_embedding.shape[0], dtype=jnp.int32)[None, :]
    ).astype(jnp.float32)
    embedded = jnp.dot(onehot, residue_type_embedding, precision=lax.Precision.HIGHEST)
    residual = single.astype(jnp.float32) + embedded[None]
    pair_norm = normalize(pair.astype(jnp.float32)).astype(jnp.bfloat16)
    bias_panel = jnp.einsum(
        "ijc,bhc->hbij", pair_norm, pair_bias_weight, preferred_element_type=jnp.float32
    )
    row_chain = lax.dynamic_slice_in_dim(chain, row_begin, row_count)
    same_strand_indicator = (row_chain[:, None] == chain[None, :]).astype(jnp.float32)
    complete_bias = lax.all_gather(bias_panel, "narrow", axis=3, tiled=True)
    score_scale = 1.0 / math.sqrt(head_dim)
    for present_segment_index in range(block_count):
        layer_head_bias = (
            complete_bias[:, present_segment_index]
            + shared_chain_score[present_segment_index][:, None, None] * same_strand_indicator[None]
        )
        normed = (
            normalize(residual).astype(jnp.bfloat16).reshape(sample_count * row_count, model_width)
        )
        query_part = jnp.dot(
            normed, query_weight[present_segment_index], preferred_element_type=jnp.float32
        ).astype(jnp.bfloat16)
        key_part = jnp.dot(
            normed, key_weight[present_segment_index], preferred_element_type=jnp.float32
        ).astype(jnp.bfloat16)
        value_part = jnp.dot(
            normed, value_weight[present_segment_index], preferred_element_type=jnp.float32
        ).astype(jnp.bfloat16)
        stacked = jnp.concatenate(
            [
                query_part.reshape(sample_count, row_count, head_count, head_dim),
                key_part.reshape(sample_count, row_count, head_count, head_dim),
                value_part.reshape(sample_count, row_count, head_count, head_dim),
            ],
            axis=-1,
        )
        regrouped = attend(stacked, layer_head_bias, score_scale)
        projected = jnp.dot(
            regrouped.reshape(sample_count * row_count, model_width),
            output_weight[present_segment_index],
            preferred_element_type=jnp.float32,
        )
        residual = residual + projected.reshape(sample_count, row_count, model_width)
    return residual.astype(jnp.bfloat16)


def solution(mesh):
    return jax.shard_map(
        shards,
        mesh=mesh,
        in_specs=(
            P("narrow", "wide", None),
            P("wide", "narrow", None),
            P("wide"),
            P(),
            P(),
            P(),
            P(),
            P(),
            P(),
            P(),
            P(),
        ),
        out_specs=P("narrow", "wide", None),
        check_vma=False,
    )
```

profile of v0, /device:TPU:0, one launch (start us, length us, event | category | flops | bytes accessed | tf_op | source)
XLA Modules:
  0.0 206.9 jit_solution(3401385552301880186)
XLA Ops:
  8.3 1.1 fusion.34
  9.4 1.2 multiply_reduce_fusion.1
  10.6 1.1 multiply_convert_fusion.1
  11.7 1.7 convolution_convert_fusion.4
  13.4 0.9 reshape.120
  14.4 1.1 copy.21
  15.5 1.7 convolution_convert_fusion.3
  17.2 0.9 reshape.121
  18.2 1.1 copy.25
  20.2 86.1 %all_gather.16 = f32[16,2,32,128]{0,3,1,2:T(8,128)} all-gather(f32[16,2,32,16]{0,3,1,2:T(8,128)S(1)} %convolution_bitcast_fusion), channel_id=1, replica_groups=mesh['wide'=4,'narrow'=8] {'narrow'}, dimensions={3}, use_global_device_ids=true | all-gather | bytes 589824 | tf_op jit(solution)/shard_map/all_gather | solution.py:76
  106.4 3.6 %fusion = (f32[16,32,128]{0,2,1:T(8,128)S(1)}, f32[16,32,128]{0,2,1:T(8,128)}) fusion(f32[16,2,32,128]{0,3,1,2:T(8,128)} %all_gather.16, f32[16]{0:T(128)S(1)} %get-tuple-element.7, f32[32,128]{1,0:T(8,128)S(1)} %compare_convert_fusion, f32[16]{0:T(128)S(1)} %get-tuple-element.8), kind=kLoop, calls=%fused_computation.1 | loop fusion | flops 262144 | bytes 1065088 | tf_op jit(solution)/shard_map/add | solution.py:80
  110.0 2.2 %copy.24 = f32[16,32,128]{2,1,0:T(8,128)S(1)} copy(f32[16,32,128]{0,2,1:T(8,128)} %get-tuple-element.6) | data formatting | bytes 524288 | tf_op jit(solution)/shard_map/add | solution.py:80
  112.2 2.4 %convolution_convert_fusion.5 = bf16[192,768]{1,0:T(8,128)(2,1)} fusion(bf16[192,768]{1,0:T(8,128)(2,1)S(1)} %bitcast.100, bf16[2,768,768]{2,1,0:T(8,128)(2,1)} %param.18), kind=kOutput, calls=%fused_computation.27 | convolution fusion | flops 226639872 | bytes 1769472 | tf_op jit(solution)/shard_map/dot_general | solution.py:86
  114.6 1.8 reshape.119
  116.5 3.7 %fusion.46 = (f32[6,16,32]{2,1,0:T(8,128)S(1)}, f32[6,16,32,128]{3,2,1,0:T(8,128)S(1)}) fusion(f32[16,32,128]{2,1,0:T(8,128)S(1)} %copy.24, bf16[6,128,16,48]{3,1,2,0:T(8,128)(2,1)} %all-gather.5.cloned.1.call-done, bf16[6,32,16,48]{3,2,1,0:T(8,128)(2,1)S(1)} %reshape.119), kind=kOutput, calls=%fused_computation.81 | convolution fusion | flops 38925312 | bytes 3321856 | tf_op jit(solution)/shard_map/aqhd,akhd->ahqk/dot_general | solution.py:29
  120.2 1.1 copy-done.1
  122.4 4.2 %fusion.5 = bf16[6,32,16,48]{3,1,2,0:T(8,128)(2,1)S(1)} fusion(bf16[6,128,16,48]{3,1,2,0:T(8,128)(2,1)} %all-gather.7.cloned.1.call-done, f32[6,16,32,128]{3,2,1,0:T(8,128)} %copy-done.1, f32[6,32,16]{1,2,0:T(8,128)S(1)} %bitcast_add_fusion.3, f32[6,16,32]{2,1,0:T(8,128)S(1)} %get-tuple-element.9, f32[6,32,16]{1,2,0:T(8,128)S(1)} %multiply_bitcast_fusion.1), kind=kOutput, calls=%fused_computation.9 | convolution fusion | flops 38977536 | bytes 3084288 | tf_op jit(solution)/shard_map/ahqk,akhd->aqhd/dot_general | solution.py:37
  126.9 1.5 dot_general.53
  128.4 2.0 fusion.47
  130.7 1.1 convolution_convert_fusion.1
  131.9 2.7 %reshape.124 = bf16[6,32,16,48]{3,2,1,0:T(8,128)(2,1)} reshape(bf16[192,768]{1,0:T(8,128)(2,1)} %convolution_convert_fusion.1) | data formatting | bytes 589824 | tf_op jit(solution)/shard_map/reshape | solution.py:98
  134.6 2.2 %copy.27 = bf16[6,32,16,48]{3,1,2,0:T(8,128)(2,1)} copy(bf16[6,32,16,48]{3,2,1,0:T(8,128)(2,1)} %reshape.124) | data formatting | bytes 589824 | tf_op jit(solution)/shard_map/reshape | solution.py:98
  137.1 2.4 %convolution_convert_fusion = bf16[192,768]{1,0:T(8,128)(2,1)} fusion(bf16[192,768]{1,0:T(8,128)(2,1)S(1)} %bitcast.96, bf16[2,768,768]{2,1,0:T(8,128)(2,1)} %param.20), kind=kOutput, calls=%fused_computation.22 | convolution fusion | flops 226639872 | bytes 1769472 | tf_op jit(solution)/shard_map/dot_general | solution.py:92
  139.5 2.7 %reshape.125 = bf16[6,32,16,48]{3,2,1,0:T(8,128)(2,1)} reshape(bf16[192,768]{1,0:T(8,128)(2,1)} %convolution_convert_fusion) | data formatting | bytes 589824 | tf_op jit(solution)/shard_map/reshape | solution.py:99
  142.2 2.3 %copy.30 = bf16[6,32,16,48]{3,1,2,0:T(8,128)(2,1)} copy(bf16[6,32,16,48]{3,2,1,0:T(8,128)(2,1)} %reshape.125) | data formatting | bytes 589824 | tf_op jit(solution)/shard_map/reshape | solution.py:99
  145.2 1.7 convolution_convert_fusion.2
  146.8 1.9 reshape.123
  148.7 15.4 %all-gather.9.cloned.1.call-done = bf16[6,128,16,48]{3,1,2,0:T(8,128)(2,1)} async-done(((bf16[6,32,16,48]{3,1,2,0:T(8,128)(2,1)}), bf16[6,128,16,48]{3,1,2,0:T(8,128)(2,1)}) %all-gather.9.cloned.1.call-update) | async-done | bytes 1179664 | tf_op jit(solution)/shard_map/all_gather | solution.py:26
  164.1 4.0 %fusion.48 = (f32[6,16,32]{2,1,0:T(8,128)S(1)}, f32[6,16,32,128]{3,2,1,0:T(8,128)S(1)}) fusion(f32[16,32,128]{2,1,0:T(8,128)S(1)} %copy.29, bf16[6,128,16,48]{3,1,2,0:T(8,128)(2,1)} %all-gather.9.cloned.1.call-done, bf16[6,32,16,48]{3,2,1,0:T(8,128)(2,1)} %reshape.123), kind=kOutput, calls=%fused_computation.83 | convolution fusion | flops 38925312 | bytes 3321856 | tf_op jit(solution)/shard_map/aqhd,akhd->ahqk/dot_general | solution.py:29
  169.1 25.0 %all-gather.11.cloned.1.call-done = bf16[6,128,16,48]{3,1,2,0:T(8,128)(2,1)} async-done(((bf16[6,32,16,48]{3,1,2,0:T(8,128)(2,1)}), bf16[6,128,16,48]{3,1,2,0:T(8,128)(2,1)}) %all-gather.11.cloned.1.call-update) | async-done | bytes 1179664 | tf_op jit(solution)/shard_map/all_gather | solution.py:27
  194.1 2.8 %fusion.3 = bf16[6,32,16,48]{3,1,2,0:T(8,128)(2,1)S(1)} fusion(bf16[6,128,16,48]{3,1,2,0:T(8,128)(2,1)} %all-gather.11.cloned.1.call-done, f32[6,16,32,128]{3,2,1,0:T(8,128)S(1)} %get-tuple-element.14, f32[6,32,16]{1,2,0:T(8,128)S(1)} %bitcast_add_fusion.2, f32[6,16,32]{2,1,0:T(8,128)S(1)} %get-tuple-element.13, f32[6,32,16]{1,2,0:T(8,128)S(1)} %multiply_bitcast_fusion), kind=kOutput, calls=%fused_computation.6 | convolution fusion | flops 38977536 | bytes 3084288 | tf_op jit(solution)/shard_map/ahqk,akhd->aqhd/dot_general | solution.py:37
  198.0 2.4 %fusion.10 = bf16[6,32,768]{2,1,0:T(8,128)(2,1)} fusion(f32[6,32,768]{2,1,0:T(8,128)S(1)} %get-tuple-element.12, bf16[6,32,768]{2,1,0:T(8,128)(2,1)S(1)} %dot_general.60, bf16[2,768,768]{2,1,0:T(8,128)(2,1)} %param.21), kind=kOutput, calls=%fused_computation.21 | convolution fusion | flops 226787328 | bytes 2359296 | tf_op jit(solution)/shard_map/dot_general | solution.py:104
  (50 shorter events, 7.4 us)
Async XLA Ops:
  6.5 0.9 copy-start
  6.5 109.9 %all-gather.5.cloned.1.call-start = ((), (), s32[]{:S(2)}) async-start(), calls=%async_computation | async-start | bytes 3932160 | tf_op jit(solution)/shard_map/all_gather | solution.py:26
  15.5 106.9 %all-gather.7.cloned.1.call-start = ((), (), s32[]{:S(2)}) async-start(), calls=%async_computation.1 | async-start | bytes 3932160 | tf_op jit(solution)/shard_map/all_gather | solution.py:27
  17.2 2.2 %copy-start.3 = (bf16[32,16,128]{2,1,0:T(8,128)(2,1)S(1)}, bf16[32,16,128]{2,1,0:T(8,128)(2,1)}, u32[]{:S(2)}) copy-start(bf16[32,16,128]{2,1,0:T(8,128)(2,1)} %param.12) | copy-start | bytes 393220
  18.2 1.7 copy-start.4
  19.3 144.8 %all-gather.9.cloned.1.call-start = ((), (), s32[]{:S(2)}) async-start(), calls=%async_computation.2 | async-start | bytes 3932160 | tf_op jit(solution)/shard_map/all_gather | solution.py:26
  20.1 86.1 %copy-start.6 = (s32[128]{0:T(128)S(1)}, s32[128]{0:T(128)}, u32[]{:S(2)}) copy-start(s32[128]{0:T(128)} %param.14) | copy-start | bytes 1540
  20.1 86.3 %copy-start.5 = (f32[2,16]{1,0:T(2,128)S(1)}, f32[2,16]{1,0:T(2,128)}, u32[]{:S(2)}) copy-start(f32[2,16]{1,0:T(2,128)} %param.17) | copy-start | bytes 388
  120.2 1.2 copy-start.1
  126.5 1.8 copy-start.2
  128.4 2.4 %copy-start.7 = (bf16[2,768,768]{2,1,0:T(8,128)(2,1)S(1)}, bf16[2,768,768]{2,1,0:T(8,128)(2,1)}, u32[]{:S(2)}) copy-start(bf16[2,768,768]{2,1,0:T(8,128)(2,1)} %param.19) | copy-start | bytes 7077892
  136.8 57.2 %all-gather.11.cloned.1.call-start = ((), (), s32[]{:S(2)}) async-start(), calls=%async_computation.3 | async-start | bytes 3932160 | tf_op jit(solution)/shard_map/all_gather | solution.py:27
Sparse Core Ops, SparseCore 0:
  15.6 31.2 all-gather.4
  48.4 28.4 all-gather.6
  137.0 27.1 all-gather.8
  165.5 28.4 all-gather.10
where the time goes:
time: 208 us; the launch traced here: 207 us
  blocking collectives  86.1 us (41%)
  waiting for transfers between devices  40.5 us (19%)
  matrix products  31.2 us (15%)
  local copies, waits for them, and re-layouts  25.6 us (12%)
  between operations  13.5 us (6%)
  other arithmetic  9.64 us (5%)
    all_gather x1, blocking collectives, shards(): complete_bias = lax.all_gather(bias_panel, 'narrow', axis=3, tiled=True)  86.1 us
    all_gather x2, waiting for transfers between devices, attend(): value_piece = lax.all_gather(value_rows, 'wide', axis=1, tiled=True)  25 us
    all_gather x2, waiting for transfers between devices, attend(): key_piece = lax.all_gather(key_rows, 'wide', axis=1, tiled=True)  15.4 us
    dot_general x2, matrix products, attend(): jnp.einsum('aqhd,akhd->ahqk', queries, key_piece, preferred_element_type=...  7.66 us
    reshape x4, local copies, waits for them, and re-layouts, shards(): value_part.reshape(sample_count, row_count, head_count, head_dim)  7.09 us
    dot_general x2, matrix products, attend(): jnp.einsum('ahqk,akhd->aqhd', weights_exp.astype(jnp.bfloat16), value_pie...  6.99 us
    reshape x4, local copies, waits for them, and re-layouts, shards(): key_part.reshape(sample_count, row_count, head_count, head_dim)  6.98 us
    dot_general x2, matrix products, shards(): jnp.dot(regrouped.reshape(sample_count * row_count, model_width), output_...  4.39 us
  transfers between devices with their start and end apart: 4, of which 2 were waited for; matrix products, arithmetic and copies ran while one was open for 17% of the time, Pallas kernels for 0%

commit v1 on v0

--- a/solution.py
+++ b/solution.py
@@ -3,6 +3,7 @@
 import jax.numpy as jnp
 from jax import lax
 from jax.sharding import PartitionSpec as P
+from jax.lax import all_gather
 
 epsilon_norm = 1e-05
 
@@ -23,8 +24,11 @@
     running_max = jnp.full((batch_count, head_count, row_count), -jnp.inf, jnp.float32)
     running_sum = jnp.zeros((batch_count, head_count, row_count), jnp.float32)
     running_out = jnp.zeros((batch_count, row_count, head_count, head_dim), jnp.float32)
-    key_piece = lax.all_gather(key_rows, "wide", axis=1, tiled=True)
-    value_piece = lax.all_gather(value_rows, "wide", axis=1, tiled=True)
+    key_piece, value_piece = jnp.split(
+        all_gather(jnp.concatenate([key_rows, value_rows], 0), "wide", axis=1, tiled=True),
+        [key_rows.shape[0]],
+        0,
+    )
     scores = (
         jnp.einsum("aqhd,akhd->ahqk", queries, key_piece, preferred_element_type=jnp.float32)
         * score_scale

time: 208 us -> 208 us (level)
  matrix products: 31.2 us -> 26.9 us
  local copies, waits for them, and re-layouts: 25.6 us -> 29.3 us
  waiting for transfers between devices: 40.5 us -> 43 us
    split x0 -> x2, local copies, waits for them, and re-layouts: none -> 7.9 us  [attend(): jnp.split(all_gather(jnp.concatenate([key_rows, value_rows], 0), 'wide',...]
    dot_general x2, matrix products: 7.66 us -> 3.64 us  [attend(): jnp.einsum('aqhd,akhd->ahqk', queries, key_piece, preferred_element_type=...]
    reshape x4 -> x2, local copies, waits for them, and re-layouts: 7.09 us -> 3.67 us  [shards(): value_part.reshape(sample_count, row_count, head_count, head_dim)]
    concatenate x0 -> x2, local copies, waits for them, and re-layouts: none -> 3.3 us  [attend(): jnp.concatenate([key_rows, value_rows], 0)]
    reshape x4 -> x2, local copies, waits for them, and re-layouts: 6.98 us -> 3.7 us  [shards(): key_part.reshape(sample_count, row_count, head_count, head_dim)]
    all_gather x4 -> x2, waiting for transfers between devices: 40.4 us -> 42.9 us  [attend(): all_gather(jnp.concatenate([key_rows, value_rows], 0), 'wide', axis=1, ti...]
  transfers between devices with their start and end apart: 4 -> 2, of which waited for: 2 -> 1; matrix products, arithmetic and copies ran while one was open for 17% -> 6% of each run, Pallas kernels for 0% -> 0%
where the time goes in v1:
time: 208 us
  blocking collectives  84.8 us (41%)
  waiting for transfers between devices  43 us (21%)
  local copies, waits for them, and re-layouts  29.3 us (14%)
  matrix products  26.9 us (13%)
  between operations  13.7 us (7%)
  other arithmetic  9.9 us (5%)
    all_gather x1, blocking collectives, shards(): complete_bias = lax.all_gather(bias_panel, 'narrow', axis=3, tiled=True)  84.8 us
    all_gather x2, waiting for transfers between devices, attend(): all_gather(jnp.concatenate([key_rows, value_rows], 0), 'wide', axis=1, ti...  42.9 us
    dot_general x2, matrix products, attend(): jnp.einsum('ahqk,akhd->aqhd', weights_exp.astype(jnp.bfloat16), value_pie...  8.05 us
    split x2, local copies, waits for them, and re-layouts, attend(): jnp.split(all_gather(jnp.concatenate([key_rows, value_rows], 0), 'wide',...  7.9 us
    dot_general x2, matrix products, shards(): jnp.dot(regrouped.reshape(sample_count * row_count, model_width), output_...  4.39 us
  transfers between devices with their start and end apart: 2, of which 1 were waited for; matrix products, arithmetic and copies ran while one was open for 6% of the time, Pallas kernels for 0%

profile of v1, /device:TPU:0, one launch (start us, length us, event | category | flops | bytes accessed | tf_op | source)
XLA Modules:
  0.0 207.6 jit_solution(5615732368874308891)
XLA Ops:
  8.3 1.1 fusion.50
  9.4 1.2 multiply_reduce_fusion.1
  10.6 1.1 multiply_convert_fusion.1
  11.7 1.7 convolution_convert_fusion.3
  13.4 0.9 reshape.121
  14.4 1.7 convolution_convert_fusion.4
  16.0 0.9 reshape.120
  17.3 1.7 copy.48
  20.8 84.8 %all_gather.10 = f32[16,2,32,128]{0,3,1,2:T(8,128)S(1)} all-gather(f32[16,2,32,16]{0,3,1,2:T(8,128)S(1)} %convolution_bitcast_fusion), channel_id=1, replica_groups=mesh['wide'=4,'narrow'=8] {'narrow'}, dimensions={3}, use_global_device_ids=true | all-gather | bytes 589824 | tf_op jit(solution)/shard_map/all_gather | solution.py:80
  105.6 1.8 fusion.8
  107.4 2.2 %copy.37 = f32[16,32,128]{2,1,0:T(8,128)S(1)} copy(f32[16,32,128]{0,2,1:T(8,128)} %get-tuple-element.10) | data formatting | bytes 524288 | tf_op jit(solution)/shard_map/add | solution.py:84
  109.6 2.4 %convolution_convert_fusion.5 = bf16[192,768]{1,0:T(8,128)(2,1)} fusion(bf16[192,768]{1,0:T(8,128)(2,1)S(1)} %bitcast.96, bf16[2,768,768]{2,1,0:T(8,128)(2,1)} %param.18), kind=kOutput, calls=%fused_computation.37 | convolution fusion | flops 226639872 | bytes 1769472 | tf_op jit(solution)/shard_map/dot_general | solution.py:90
  112.0 1.8 reshape.119
  113.9 4.0 %fusion.63 = (bf16[6,128,16,48]{3,2,0,1:T(8,128)(2,1)S(1)}, bf16[6,128,16,48]{3,2,0,1:T(8,128)(2,1)S(1)}) fusion(bf16[12,128,16,48]{3,2,0,1:T(8,128)(2,1)} %all-gather.3.cloned.1.call-done), kind=kLoop, calls=%fused_computation.92 | loop fusion | bytes 4718592 | tf_op jit(solution)/shard_map/split | solution.py:27
  117.8 1.8 fusion.64
  119.7 0.9 fusion.22
  120.6 4.1 %fusion.13 = bf16[6,32,16,48]{3,1,2,0:T(8,128)(2,1)S(1)} fusion(bf16[6,128,16,48]{3,2,0,1:T(8,128)(2,1)S(1)} %get-tuple-element.8, f32[6,16,32,128]{3,2,1,0:T(8,128)S(1)} %get-tuple-element.14, f32[6,32,16]{1,2,0:T(8,128)S(1)} %bitcast_add_fusion.3, f32[6,16,32]{2,1,0:T(8,128)S(1)} %get-tuple-element.13, f32[6,32,16]{1,2,0:T(8,128)S(1)} %multiply_bitcast_fusion.1), kind=kOutput, calls=%fused_computation.19 | convolution fusion | flops 38977536 | bytes 3084288 | tf_op jit(solution)/shard_map/ahqk,akhd->aqhd/dot_general | solution.py:41
  125.1 1.5 dot_general.53
  126.6 2.0 fusion.65
  129.0 1.1 convolution_convert_fusion
  130.6 1.1 convolution_convert_fusion.1
  131.7 2.7 %reshape.125 = bf16[6,32,16,48]{3,2,1,0:T(8,128)(2,1)} reshape(bf16[192,768]{1,0:T(8,128)(2,1)} %convolution_convert_fusion) | data formatting | bytes 589824 | tf_op jit(solution)/shard_map/reshape | solution.py:103
  134.4 2.8 %reshape.124 = bf16[6,32,16,48]{3,2,1,0:T(8,128)(2,1)} reshape(bf16[192,768]{1,0:T(8,128)(2,1)} %convolution_convert_fusion.1) | data formatting | bytes 589824 | tf_op jit(solution)/shard_map/reshape | solution.py:102
  137.2 1.7 pad_maximum_fusion.1
  138.9 1.6 copy.49
  141.1 1.7 convolution_convert_fusion.2
  142.8 0.9 reshape.123
  143.7 42.9 %all-gather.5.cloned.1.call-done = bf16[12,128,16,48]{3,2,0,1:T(8,128)(2,1)} async-done(((bf16[12,32,16,48]{3,2,0,1:T(8,128)(2,1)}), bf16[12,128,16,48]{3,2,0,1:T(8,128)(2,1)}) %all-gather.5.cloned.1.call-update) | async-done | bytes 2359312 | tf_op jit(solution)/shard_map/all_gather | solution.py:28
  186.6 3.9 %fusion.62 = (bf16[6,128,16,48]{3,2,0,1:T(8,128)(2,1)S(1)}, bf16[6,128,16,48]{3,2,0,1:T(8,128)(2,1)S(1)}) fusion(bf16[12,128,16,48]{3,2,0,1:T(8,128)(2,1)} %all-gather.5.cloned.1.call-done), kind=kLoop, calls=%fused_computation.91 | loop fusion | bytes 4718592 | tf_op jit(solution)/shard_map/split | solution.py:27
  190.6 1.8 fusion.66
  193.4 3.9 %fusion.11 = bf16[6,32,16,48]{3,1,2,0:T(8,128)(2,1)S(1)} fusion(bf16[6,128,16,48]{3,2,0,1:T(8,128)(2,1)S(1)} %get-tuple-element.6, f32[6,16,32,128]{3,2,1,0:T(8,128)S(1)} %get-tuple-element.18, f32[6,32,16]{1,2,0:T(8,128)S(1)} %bitcast_add_fusion.2, f32[6,16,32]{2,1,0:T(8,128)S(1)} %get-tuple-element.17, f32[6,32,16]{1,2,0:T(8,128)S(1)} %multiply_bitcast_fusion), kind=kOutput, calls=%fused_computation.16 | convolution fusion | flops 38977536 | bytes 3084288 | tf_op jit(solution)/shard_map/ahqk,akhd->aqhd/dot_general | solution.py:41
  198.4 2.4 %fusion.26 = bf16[6,32,768]{2,1,0:T(8,128)(2,1)} fusion(f32[6,32,768]{2,1,0:T(8,128)S(1)} %get-tuple-element.16, bf16[6,32,768]{2,1,0:T(8,128)(2,1)S(1)} %dot_general.60, bf16[2,768,768]{2,1,0:T(8,128)(2,1)} %param.21), kind=kOutput, calls=%fused_computation.31 | convolution fusion | flops 226787328 | bytes 2359296 | tf_op jit(solution)/shard_map/dot_general | solution.py:108
  (46 shorter events, 7.6 us)
Async XLA Ops:
  6.5 0.9 copy-start
  6.5 107.3 %all-gather.3.cloned.1.call-start = ((), (), s32[]{:S(2)}) async-start(), calls=%async_computation | async-start | bytes 7864320 | tf_op jit(solution)/shard_map/all_gather | solution.py:28
  19.0 0.7 copy-start.5
  19.0 0.9 copy-start.2
  19.0 1.3 copy-start.4
  19.0 1.4 copy-start.3
  19.0 167.6 %all-gather.5.cloned.1.call-start = ((), (), s32[]{:S(2)}) async-start(), calls=%async_computation.1 | async-start | bytes 7864320 | tf_op jit(solution)/shard_map/all_gather | solution.py:28
  124.8 1.8 copy-start.1
  126.6 2.4 %copy-start.6 = (bf16[2,768,768]{2,1,0:T(8,128)(2,1)S(1)}, bf16[2,768,768]{2,1,0:T(8,128)(2,1)}, u32[]{:S(2)}) copy-start(bf16[2,768,768]{2,1,0:T(8,128)(2,1)} %param.20) | copy-start | bytes 7077892
  128.8 1.8 copy-start.7
Sparse Core Ops, SparseCore 0:
  19.1 49.0 all-gather.2
  140.6 45.9 all-gather.4
